TPU v7x, 32 devices: a whole 2x2x4 slice. The times are simulated.
32 devices in a mesh: section: 4 (over x, core), tensor: 4 (over z), dp: 2 (over y).
Axes of the slice: x: 2, y: 2, z: 4, core: 2. Of those that a mesh axis runs over, the one named last changes fastest.
Arguments:
- layer_in: bfloat16 [2, 2, 4, 2, 128, 2560], P(None, None, 'section', 'dp', 'tensor'), may hold values from -6 to 6
- carry_in: bfloat16 [2, 4, 2, 128, 2560], P(None, 'section', 'dp', 'tensor'), may hold values from -6 to 6
- top_grad: bfloat16 [1, 2, 128, 2560], P(None, 'dp', 'tensor'), may hold values from -6 to 6
- w_qkv: bfloat16 [2, 4, 2560, 2560], P(None, 'section', None, 'tensor'), may hold values from -1 to 1
- w_out: bfloat16 [2, 4, 2048, 2560], P(None, 'section', 'tensor'), may hold values from -0.125 to 0.125
- gain: float32 [2, 4, 2560], P(None, 'section'), may hold values from 0.5 to 1.5
Outputs:
- unit_grads: bfloat16 [2, 2, 4, 2, 128, 2560], P(None, None, 'section', 'dp', 'tensor')
- grad_qkv: bfloat16 [2, 4, 2560, 2560], P(None, 'section', 'dp', 'tensor')
- grad_out: bfloat16 [2, 4, 2048, 2560], P(None, 'section', ('tensor', 'dp'))
- grad_gain: float32 [2, 4, 2560], P(None, 'section')
All inputs are finite; a program needn't handle non-finite values.
Results may differ from a plain program's by a relative error of at most 0.022.
The roundings to bfloat16 on the way count: a program that leaves them out, or rounds other values in their place, can miss the bound.
Values may be sent and summed in bfloat16 or wider, within the bound.
A program may use at most 128 MiB of HBM per device.

v0:
```python
import math
import jax
import jax.numpy as jnp
from jax import lax
from jax.sharding import PartitionSpec as P

KV = 4
HD = 64
GROUP = 8
epsilon = 1e-06
rope_base = 1000000.0


def from_behind(value, axis, steps):
    count = lax.axis_size(axis)
    first, last = (max(0, -steps), min(count, count - steps))
    return lax.ppermute(value, axis, [(source, source + steps) for source in range(first, last)])


def rope_tables(length, head_width):
    half_width = head_width // 2
    exponent = jnp.arange(half_width, dtype=jnp.float32) * (2.0 / head_width)
    frequency = rope_base ** (-exponent)
    angle = jnp.arange(length, dtype=jnp.float32)[:, None] * frequency[None, :]
    return (jnp.cos(angle), jnp.sin(angle))


def rotate(values, cosine_table, sine_table, direction):
    half_width = values.shape[-1] // 2
    table_shape = (values.shape[0],) + (1,) * (values.ndim - 2) + (half_width,)
    cosine = cosine_table.reshape(table_shape)
    sine_part = direction * sine_table.reshape(table_shape)
    lower_half = values[..., :half_width]
    upper_half = values[..., half_width:]
    return jnp.concatenate(
        [
            lower_half * cosine - upper_half * sine_part,
            upper_half * cosine + lower_half * sine_part,
        ],
        axis=-1,
    )


def local(layer_in, carry_in, top_grad, w_qkv, w_out, gain):
    ticks = layer_in.shape[0]
    own_rows = layer_in.shape[4]
    length = own_rows * lax.axis_size("tensor")
    kv_local = KV // lax.axis_size("tensor")
    section_index = lax.axis_index("section")
    at_first = section_index == 0
    at_last = section_index == lax.axis_size("section") - 1
    cosine_table, sine_table = rope_tables(length, HD)
    score_scale = 1.0 / math.sqrt(HD)
    causal_mask = jnp.arange(length)[:, None] >= jnp.arange(length)[None, :]
    layer_rows = layer_in[:, :, 0, 0]
    carried = carry_in[:, 0, 0]
    fresh_grads = top_grad[:, 0]
    weight_qkv = w_qkv[:, 0]
    weight_out = w_out[:, 0]
    gain_rows = gain[:, 0]
    contract_rows = (((0,), (0,)), ((), ()))
    contract_cols = (((1,), (1,)), ((), ()))
    qkv_sums = [
        jnp.zeros(weight_qkv.shape[1:], jnp.float32),
        jnp.zeros(weight_qkv.shape[1:], jnp.float32),
    ]
    out_sums = [
        jnp.zeros(weight_out.shape[1:], jnp.float32),
        jnp.zeros(weight_out.shape[1:], jnp.float32),
    ]
    gain_totals = [
        jnp.zeros(gain_rows.shape[1:], jnp.float32),
        jnp.zeros(gain_rows.shape[1:], jnp.float32),
    ]

    def apply_weights(member, stored):
        normed, grad_full, attended, grad_projected = stored
        qkv_sums[member] = qkv_sums[member] + lax.dot_general(
            normed, grad_projected, contract_rows, preferred_element_type=jnp.float32
        )
        out_sums[member] = out_sums[member] + lax.dot_general(
            attended, grad_full, contract_rows, preferred_element_type=jnp.float32
        )

    inputs = [carried[0], carried[1]]
    per_tick = []
    for position in range(ticks):
        outcome = [None, None]
        pending_members = []
        pending_saved = []
        for member in (1, 0):
            layer_part = layer_rows[position, member]
            grad_output = inputs[member]
            inputs_float = layer_part.astype(jnp.float32)
            inverse = lax.rsqrt(
                jnp.mean(inputs_float * inputs_float, axis=-1, keepdims=True) + epsilon
            )
            unit_rows = inputs_float * inverse
            normed_own = (unit_rows * gain_rows[member]).astype(jnp.bfloat16)
            input_normed = lax.all_gather(normed_own, "tensor", axis=0, tiled=True)
            input_grad_full = lax.all_gather(grad_output, "tensor", axis=0, tiled=True)
            projected = jnp.dot(
                input_normed, weight_qkv[member], preferred_element_type=jnp.float32
            )
            projected = projected.reshape(length, kv_local, GROUP + 2, HD)
            query_rot = rotate(projected[:, :, :GROUP], cosine_table, sine_table, 1.0).astype(
                jnp.bfloat16
            )
            key_rot = rotate(projected[:, :, GROUP], cosine_table, sine_table, 1.0).astype(
                jnp.bfloat16
            )
            value_rows = projected[:, :, GROUP + 1].astype(jnp.bfloat16)
            scores = (
                jnp.einsum("tkgd,ukd->kgtu", query_rot, key_rot, preferred_element_type=jnp.float32)
                * score_scale
            )
            scores = jnp.where(causal_mask, scores, -1e30)
            exponentials = jnp.exp(scores - jnp.max(scores, axis=-1, keepdims=True))
            softmax_rows = exponentials / jnp.sum(exponentials, axis=-1, keepdims=True)
            softmax_low = softmax_rows.astype(jnp.bfloat16)
            input_attended = jnp.einsum(
                "kgtu,ukd->tkgd", softmax_low, value_rows, preferred_element_type=jnp.float32
            )
            input_attended = input_attended.astype(jnp.bfloat16).reshape(
                length, kv_local * GROUP * HD
            )
            grad_attended = lax.dot_general(
                input_grad_full,
                weight_out[member],
                contract_cols,
                preferred_element_type=jnp.float32,
            ).astype(jnp.bfloat16)
            grad_heads = grad_attended.reshape(length, kv_local, GROUP, HD)
            grad_softmax = jnp.einsum(
                "tkgd,ukd->kgtu", grad_heads, value_rows, preferred_element_type=jnp.float32
            )
            row_total = jnp.sum(softmax_rows * grad_softmax, axis=-1, keepdims=True)
            grad_scores = (softmax_rows * (grad_softmax - row_total) * score_scale).astype(
                jnp.bfloat16
            )
            grad_value = jnp.einsum(
                "kgtu,tkgd->ukd", softmax_low, grad_heads, preferred_element_type=jnp.float32
            )
            grad_query = rotate(
                jnp.einsum(
                    "kgtu,ukd->tkgd", grad_scores, key_rot, preferred_element_type=jnp.float32
                ),
                cosine_table,
                sine_table,
                -1.0,
            )
            grad_key = rotate(
                jnp.einsum(
                    "kgtu,tkgd->ukd", grad_scores, query_rot, preferred_element_type=jnp.float32
                ),
                cosine_table,
                sine_table,
                -1.0,
            )
            input_grad_projected = jnp.concatenate(
                [grad_query, grad_key[:, :, None], grad_value[:, :, None]], axis=2
            )
            input_grad_projected = input_grad_projected.reshape(
                length, kv_local * (GROUP + 2) * HD
            ).astype(jnp.bfloat16)
            grad_normed = lax.psum_scatter(
                lax.dot_general(
                    input_grad_projected,
                    weight_qkv[member],
                    contract_cols,
                    preferred_element_type=jnp.float32,
                ).astype(jnp.bfloat16),
                "tensor",
                scatter_dimension=0,
                tiled=True,
            ).astype(jnp.float32)
            grad_unit = grad_normed * gain_rows[member]
            grad_rows = inverse * (
                grad_unit - unit_rows * jnp.mean(grad_unit * unit_rows, axis=-1, keepdims=True)
            )
            grad_input = (grad_output.astype(jnp.float32) + grad_rows).astype(jnp.bfloat16)
            grad_scale = jnp.sum(grad_normed * unit_rows, axis=0)
            grad_input, stored, grad_scale = (
                grad_input,
                (input_normed, input_grad_full, input_attended, input_grad_projected),
                grad_scale,
            )
            outcome[member] = grad_input
            gain_totals[member] = gain_totals[member] + grad_scale
            pending_members.append(member)
            pending_saved.append(stored)
        if position + 1 < ticks:
            upward = from_behind(outcome[1], "section", 1)
            downward = from_behind(outcome[0], "section", -1)
            pending_saved, upward, downward = lax.optimization_barrier(
                (pending_saved, upward, downward)
            )
            inputs = [
                jnp.where(at_last, outcome[1], downward),
                jnp.where(at_first, fresh_grads[position], upward),
            ]
        for member, stored in zip(pending_members, pending_saved):
            apply_weights(member, stored)
        per_tick.append(jnp.stack(outcome))
    grad_qkv_all, grad_out_all = (
        lax.psum_scatter(
            jnp.stack(qkv_sums).astype(jnp.bfloat16), "dp", scatter_dimension=1, tiled=True
        ).astype(jnp.float32),
        lax.psum_scatter(
            jnp.stack(out_sums).astype(jnp.bfloat16), "dp", scatter_dimension=1, tiled=True
        ).astype(jnp.float32),
    )
    gain_total = lax.psum(jnp.stack(gain_totals), ("tensor", "dp"))
    unit_grads = jnp.stack(per_tick)[:, :, None, None]
    return (
        unit_grads,
        grad_qkv_all.astype(jnp.bfloat16)[:, None],
        grad_out_all.astype(jnp.bfloat16)[:, None],
        gain_total[:, None],
    )


def solution(mesh):
    in_specs = (
        P(None, None, "section", "dp", "tensor", None),
        P(None, "section", "dp", "tensor", None),
        P(None, "dp", "tensor", None),
        P(None, "section", None, "tensor"),
        P(None, "section", "tensor", None),
        P(None, "section", None),
    )
    out_specs = (
        P(None, None, "section", "dp", "tensor", None),
        P(None, "section", "dp", "tensor"),
        P(None, "section", ("tensor", "dp"), None),
        P(None, "section", None),
    )
    return jax.shard_map(local, mesh=mesh, in_specs=in_specs, out_specs=out_specs, check_vma=False)
```

profile of v0, /device:TPU:0, one launch (start us, length us, event | category | flops | bytes accessed | tf_op | source)
XLA Modules:
  0.0 479.4 jit_solution(15156333436391977317)
XLA Ops:
  7.3 1.2 fusion.91
  10.1 1.7 fusion.181
  11.8 19.7 %all-gather = bf16[1,1,1,128,2560]{4,3,2,1,0:T(8,128)(2,1)S(1)} all-gather(bf16[1,1,1,32,2560]{4,3,2,1,0:T(8,128)(2,1)S(1)} %get-tuple-element.68), channel_id=2, replica_groups=mesh['section'=4,'tensor'=4,'dp'=2] {'tensor'}, dimensions={3}, use_global_device_ids=true | all-gather | bytes 819200 | tf_op jit(solution)/shard_map/all_gather | solution.py:101
  32.3 2.7 fusion.32
  35.4 17.5 %all_gather.24 = bf16[128,2560]{1,0:T(8,128)(2,1)} all-gather(bf16[32,2560]{1,0:T(8,128)(2,1)S(1)} %get-tuple-element.58), channel_id=1, replica_groups=mesh['section'=4,'tensor'=4,'dp'=2] {'tensor'}, dimensions={0}, use_global_device_ids=true | all-gather | bytes 819200 | tf_op jit(solution)/shard_map/all_gather | solution.py:100
  52.9 16.7 %all_gather.26 = bf16[128,2560]{1,0:T(8,128)(2,1)} all-gather(bf16[32,2560]{1,0:T(8,128)(2,1)S(1)} %get-tuple-element.59), channel_id=1, replica_groups=mesh['section'=4,'tensor'=4,'dp'=2] {'tensor'}, dimensions={0}, use_global_device_ids=true | all-gather | bytes 819200 | tf_op jit(solution)/shard_map/all_gather | solution.py:100
  69.6 6.2 %slice_bitcast_fusion.1 = (bf16[640,2560]{0,1:T(8,128)(2,1)}, bf16[640,2560]{0,1:T(8,128)(2,1)}) fusion(bf16[2,1,2560,640]{3,2,1,0:T(8,128)(2,1)} %param.9), kind=kLoop, calls=%fused_computation.30 | loop fusion | bytes 13107200 | tf_op jit(solution)/shard_map/dot_general | solution.py:102
  75.9 4.0 copy.39
  79.9 2.1 convolution_bitcast_fusion.7
  82.7 5.7 %copy.44 = bf16[640,2560]{1,0:T(8,128)(2,1)} copy(bf16[640,2560]{0,1:T(8,128)(2,1)} %get-tuple-element.51) | data formatting | bytes 6553600 | tf_op jit(solution)/shard_map/dot_general | solution.py:102
  88.4 3.2 convolution_bitcast_fusion.6
  95.4 15.2 %all-gather.1 = bf16[1,1,1,128,2560]{4,3,2,1,0:T(8,128)(2,1)S(1)} all-gather(bf16[1,1,1,32,2560]{4,3,2,1,0:T(8,128)(2,1)S(1)} %copy-done.33), channel_id=3, replica_groups=mesh['section'=4,'tensor'=4,'dp'=2] {'tensor'}, dimensions={3}, use_global_device_ids=true | all-gather | bytes 819200 | tf_op jit(solution)/shard_map/all_gather | solution.py:101
  110.6 0.9 copy-done.13
  111.5 3.4 fusion.38
  114.8 1.7 copy.45
  116.5 1.2 fusion.183
  117.9 1.2 convolution_bitcast_fusion.16
  119.2 1.0 multiply_reduce_fusion.2
  123.0 4.0 convolution_convert_fusion.2
  127.1 1.3 convolution_bitcast_fusion.18
  129.2 4.0 convolution_convert_fusion.3
  133.2 2.0 convolution_convert_fusion.6
  135.2 1.9 convolution_convert_fusion.7
  137.2 13.4 %reduce-scatter.9.cloned.1.call-done = bf16[32,2560]{1,0:T(8,128)(2,1)} async-done(((bf16[128,2560]{1,0:T(8,128)(2,1)}), bf16[32,2560]{1,0:T(8,128)(2,1)}) %reduce-scatter.9.cloned.1.call-update) | async-done | bytes 163856 | tf_op jit(solution)/shard_map/reduce_scatter | solution.py:166
  150.5 24.1 %reduce-scatter.7.cloned.1.call-done = bf16[32,2560]{1,0:T(8,128)(2,1)} async-done(((bf16[128,2560]{1,0:T(8,128)(2,1)}), bf16[32,2560]{1,0:T(8,128)(2,1)}) %reduce-scatter.7.cloned.1.call-update) | async-done | bytes 163856 | tf_op jit(solution)/shard_map/reduce_scatter | solution.py:166
  174.7 2.3 fusion.90
  177.1 1.7 fusion.87
  178.8 16.5 %all_gather.30 = bf16[128,2560]{1,0:T(8,128)(2,1)S(1)} all-gather(bf16[32,2560]{1,0:T(8,128)(2,1)S(1)} %get-tuple-element.54), channel_id=1, replica_groups=mesh['section'=4,'tensor'=4,'dp'=2] {'tensor'}, dimensions={0}, use_global_device_ids=true | all-gather | bytes 819200 | tf_op jit(solution)/shard_map/all_gather | solution.py:100
  195.3 1.0 convolution_bitcast_fusion.4
  196.4 15.8 %all_gather.28 = bf16[128,2560]{1,0:T(8,128)(2,1)S(1)} all-gather(bf16[32,2560]{1,0:T(8,128)(2,1)S(1)} %get-tuple-element.55), channel_id=1, replica_groups=mesh['section'=4,'tensor'=4,'dp'=2] {'tensor'}, dimensions={0}, use_global_device_ids=true | all-gather | bytes 819200 | tf_op jit(solution)/shard_map/all_gather | solution.py:100
  212.2 1.0 convolution_bitcast_fusion.5
  213.4 1.4 collective-permute-start.1
  214.8 3.0 collective-permute-start
  218.4 0.9 convolution_convert_fusion.5
  221.0 17.3 %all_gather.29 = bf16[128,2560]{1,0:T(8,128)(2,1)S(1)} all-gather(bf16[32,2560]{1,0:T(8,128)(2,1)S(1)} %broadcast_select_fusion), channel_id=1, replica_groups=mesh['section'=4,'tensor'=4,'dp'=2] {'tensor'}, dimensions={0}, use_global_device_ids=true | all-gather | bytes 819200 | tf_op jit(solution)/shard_map/all_gather | solution.py:101
  238.3 0.9 copy-done.15
  239.3 1.0 fusion.35
  240.4 1.0 multiply_reduce_fusion.1
  242.4 0.9 convolution_bitcast_fusion.9
  244.0 16.7 %all_gather.31 = bf16[128,2560]{1,0:T(8,128)(2,1)S(1)} all-gather(bf16[32,2560]{1,0:T(8,128)(2,1)S(1)} %bitcast_select_fusion), channel_id=1, replica_groups=mesh['section'=4,'tensor'=4,'dp'=2] {'tensor'}, dimensions={0}, use_global_device_ids=true | all-gather | bytes 819200 | tf_op jit(solution)/shard_map/all_gather | solution.py:101
  261.5 3.5 fusion.41
  265.0 1.7 copy.55
  266.8 1.3 convolution_bitcast_fusion.12
  268.1 1.3 multiply_reduce_fusion
  272.2 2.0 convolution_convert_fusion
  274.3 1.0 convolution_convert_fusion.4
  276.0 1.2 convolution_bitcast_fusion.14
  277.3 4.0 convolution_convert_fusion.1
  281.2 3.2 fusion.189
  284.5 3.4 fusion.3
  289.0 0.8 fusion.2
  289.9 2.7 pad_maximum_fusion.1
  293.7 1.0 fusion.186
  294.8 1.0 fusion
  295.9 1.0 fusion.187
  297.0 1.0 fusion.1
  298.0 3.4 pad_maximum_fusion
  302.5 19.2 %reduce-scatter.11.cloned.1.call-done = bf16[32,2560]{1,0:T(8,128)(2,1)} async-done(((bf16[128,2560]{1,0:T(8,128)(2,1)}), bf16[32,2560]{1,0:T(8,128)(2,1)}) %reduce-scatter.11.cloned.1.call-update) | async-done | bytes 163856 | tf_op jit(solution)/shard_map/reduce_scatter | solution.py:166
  321.7 1.4 fusion.98
  323.2 36.0 %psum.7 = f32[2,1,2560]{2,1,0:T(1,128)} all-reduce(f32[2,1,2560]{2,1,0:T(1,128)S(1)} %broadcast_in_dim.33), channel_id=1, replica_groups=mesh['section'=4,'tensor'=4,'dp'=2] {'tensor','dp'}, use_global_device_ids=true, to_apply=%region_30.31 | all-reduce | flops 5120 | bytes 40960 | tf_op jit(solution)/shard_map/psum | solution.py:213
  359.2 1.2 fusion.116
  360.5 0.9 maximum_bitcast_fusion
  361.4 28.5 %reduce-scatter.17.cloned.1.call-done = bf16[2,256,2560]{2,1,0:T(8,128)(2,1)} async-done(((bf16[2,512,2560]{2,1,0:T(8,128)(2,1)}), bf16[2,256,2560]{2,1,0:T(8,128)(2,1)}) %reduce-scatter.17.cloned.1.call-update) | async-done | bytes 2621456 | tf_op jit(solution)/shard_map/reduce_scatter | solution.py:209
  389.9 82.6 %reduce-scatter.15.cloned.1.call-done = bf16[2,1280,640]{2,1,0:T(8,128)(2,1)} async-done(((bf16[2,2560,640]{2,1,0:T(8,128)(2,1)}), bf16[2,1280,640]{2,1,0:T(8,128)(2,1)}) %reduce-scatter.15.cloned.1.call-update) | async-done | bytes 3276816 | tf_op jit(solution)/shard_map/reduce_scatter | solution.py:206
  (287 shorter events, 22.8 us)
Async XLA Ops:
  7.2 28.0 %copy-start.1 = (bf16[2,2,1,1,32,2560]{5,4,3,2,1,0:T(8,128)(2,1)S(1)}, bf16[2,2,1,1,32,2560]{5,4,3,2,1,0:T(8,128)(2,1)}, u32[]{:S(2)}) copy-start(bf16[2,2,1,1,32,2560]{5,4,3,2,1,0:T(8,128)(2,1)} %param.6) | copy-start | bytes 1966084
  7.2 143.4 %reduce-scatter.9.cloned.1.call-start = ((), (), s32[]{:S(2)}) async-start(), calls=%async_computation.7 | async-start | bytes 819200 | tf_op jit(solution)/shard_map/reduce_scatter | solution.py:166
  7.2 84.4 %copy-start.88 = (f32[32]{0:T(128)}, f32[32]{0:T(128)S(1)}, u32[]{:S(2)}) copy-start(f32[32]{0:T(128)S(1)} %negate_power_fusion) | copy-start | bytes 388
  7.3 85.9 %copy-start.49 = (pred[128,128]{0,1:T(8,128)(4,1)}, pred[128,128]{0,1:T(8,128)(4,1)S(1)}, u32[]{:S(2)}) copy-start(pred[128,128]{0,1:T(8,128)(4,1)S(1)} %iota_compare_fusion) | copy-start | bytes 49156
  9.3 26.1 %copy-start.42 = (f32[2560]{0:T(1024)}, f32[2560]{0:T(1024)S(1)}, u32[]{:S(2)}) copy-start(f32[2560]{0:T(1024)S(1)} %get-tuple-element.49) | copy-start | bytes 30724
  10.1 82.3 %copy-start.45 = (f32[128,32]{0,1:T(8,128)}, f32[128,32]{0,1:T(8,128)S(1)}, u32[]{:S(2)}) copy-start(f32[128,32]{0,1:T(8,128)S(1)} %get-tuple-element.112) | copy-start | bytes 49156
  10.1 82.3 %copy-start.59 = (f32[128,32]{0,1:T(8,128)}, f32[128,32]{0,1:T(8,128)S(1)}, u32[]{:S(2)}) copy-start(f32[128,32]{0,1:T(8,128)S(1)} %get-tuple-element.111) | copy-start | bytes 49156
  35.1 58.4 %copy-start.63 = (bf16[128,512]{0,1:T(8,128)(2,1)}, bf16[128,512]{0,1:T(8,128)(2,1)S(1)}, u32[]{:S(2)}) copy-start(bf16[128,512]{0,1:T(8,128)(2,1)S(1)} %copy.40) | copy-start | bytes 393220
  35.2 40.7 %copy-start.92 = (f32[32]{0:T(128)}, f32[32]{0:T(128)S(1)}, u32[]{:S(2)}) copy-start(f32[32]{0:T(128)S(1)} %get-tuple-element.129) | copy-start | bytes 388
  35.2 40.7 %copy-start.94 = (f32[32]{0:T(128)}, f32[32]{0:T(128)S(1)}, u32[]{:S(2)}) copy-start(f32[32]{0:T(128)S(1)} %get-tuple-element.130) | copy-start | bytes 388
  88.4 4.0 copy-start.26
  91.6 3.8 copy-start.27
  116.5 3.8 copy-start.40
  116.5 3.9 copy-start.41
  122.3 4.8 copy-start.80
  122.3 4.8 copy-start.81
  123.0 5.5 %copy-start.54 = (bf16[128,1,8,32]{0,3,2,1:T(8,128)(2,1)S(1)}, bf16[128,1,8,32]{0,3,2,1:T(8,128)(2,1)}, u32[]{:S(2)}) copy-start(bf16[128,1,8,32]{0,3,2,1:T(8,128)(2,1)} %get-tuple-element.74) | copy-start | bytes 196612
  123.0 5.5 %copy-start.55 = (bf16[128,1,8,32]{0,3,2,1:T(8,128)(2,1)S(1)}, bf16[128,1,8,32]{0,3,2,1:T(8,128)(2,1)}, u32[]{:S(2)}) copy-start(bf16[128,1,8,32]{0,3,2,1:T(8,128)(2,1)} %get-tuple-element.75) | copy-start | bytes 196612
  127.0 47.6 %reduce-scatter.7.cloned.1.call-start = ((), (), s32[]{:S(2)}) async-start(), calls=%async_computation.6 | async-start | bytes 819200 | tf_op jit(solution)/shard_map/reduce_scatter | solution.py:166
  128.5 4.8 copy-start.83
  129.2 6.0 %copy-start.77 = (f32[8,128]{1,0:T(8,128)S(1)}, f32[8,128]{1,0:T(8,128)}, u32[]{:S(2)}) copy-start(f32[8,128]{1,0:T(8,128)} %copy-done.76) | copy-start | bytes 12292
  129.2 6.0 %copy-start.86 = (f32[8,128]{1,0:T(8,128)S(1)}, f32[8,128]{1,0:T(8,128)}, u32[]{:S(2)}) copy-start(f32[8,128]{1,0:T(8,128)} %copy-done.85) | copy-start | bytes 12292
  133.1 41.5 %copy-start.43 = (f32[2560]{0:T(1024)S(1)}, f32[2560]{0:T(1024)}, u32[]{:S(2)}) copy-start(f32[2560]{0:T(1024)} %copy-done.42) | copy-start | bytes 30724
  133.2 41.5 %copy-start.93 = (f32[32]{0:T(128)S(1)}, f32[32]{0:T(128)}, u32[]{:S(2)}) copy-start(f32[32]{0:T(128)} %copy-done.92) | copy-start | bytes 388
  133.2 41.5 %copy-start.95 = (f32[32]{0:T(128)S(1)}, f32[32]{0:T(128)}, u32[]{:S(2)}) copy-start(f32[32]{0:T(128)} %copy-done.94) | copy-start | bytes 388
  133.2 169.3 %reduce-scatter.13.cloned.1.call-start = ((), (), s32[]{:S(2)}) async-start(), calls=%async_computation.9 | async-start | bytes 819200 | tf_op jit(solution)/shard_map/reduce_scatter | solution.py:166
  174.7 20.7 %copy-start = (bf16[640,2560]{1,0:T(8,128)(2,1)S(1)}, bf16[640,2560]{1,0:T(8,128)(2,1)}, u32[]{:S(2)}) copy-start(bf16[640,2560]{1,0:T(8,128)(2,1)} %copy.44) | copy-start | bytes 9830404
  177.0 19.3 %copy-start.96 = (f32[32]{0:T(128)}, f32[32]{0:T(128)S(1)}, u32[]{:S(2)}) copy-start(f32[32]{0:T(128)S(1)} %add_rsqrt_fusion) | copy-start | bytes 388
  177.0 19.3 %copy-start.98 = (f32[32]{0:T(128)}, f32[32]{0:T(128)S(1)}, u32[]{:S(2)}) copy-start(f32[32]{0:T(128)S(1)} %add_rsqrt_fusion.1) | copy-start | bytes 388
  178.8 34.6 %copy-start.31 = (bf16[32,2560]{1,0:T(8,128)(2,1)}, bf16[32,2560]{1,0:T(8,128)(2,1)S(1)}, u32[]{:S(2)}) copy-start(bf16[32,2560]{1,0:T(8,128)(2,1)S(1)} %get-tuple-element.52) | copy-start | bytes 491524
  178.8 41.5 %copy-start.19 = (bf16[32,2560]{1,0:T(8,128)(2,1)}, bf16[32,2560]{1,0:T(8,128)(2,1)S(1)}, u32[]{:S(2)}) copy-start(bf16[32,2560]{1,0:T(8,128)(2,1)S(1)} %get-tuple-element.53) | copy-start | bytes 491524
  195.3 17.9 %copy-start.3 = (bf16[128,2560]{1,0:T(8,128)(2,1)}, bf16[128,2560]{1,0:T(8,128)(2,1)S(1)}, u32[]{:S(2)}) copy-start(bf16[128,2560]{1,0:T(8,128)(2,1)S(1)} %all_gather.30) | copy-start | bytes 1966084
  195.3 43.9 %slice-start.2 = ((s8[5242880]{0:T(1024)(128)(4,1)}), s8[1048576]{0:T(1024)(128)(4,1)S(1)}, s32[]{:S(2)}) async-start(s8[5242880]{0:T(1024)(128)(4,1)} %bitcast.493), calls=%async_computation.14 | async-start | bytes 2097152
  196.4 17.0 %copy-start.28 = (f32[128,1,10,64]{0,3,2,1:T(8,128)}, f32[128,1,10,64]{0,3,2,1:T(8,128)S(1)}, u32[]{:S(2)}) copy-start(f32[128,1,10,64]{0,3,2,1:T(8,128)S(1)} %convolution_bitcast_fusion.4) | copy-start | bytes 983044
  196.4 16.9 %copy-start.47 = (f32[128,32]{0,1:T(8,128)S(1)}, f32[128,32]{0,1:T(8,128)}, u32[]{:S(2)}) copy-start(f32[128,32]{0,1:T(8,128)} %copy-done.45) | copy-start | bytes 49156
  196.4 16.9 %copy-start.60 = (f32[128,32]{0,1:T(8,128)S(1)}, f32[128,32]{0,1:T(8,128)}, u32[]{:S(2)}) copy-start(f32[128,32]{0,1:T(8,128)} %copy-done.59) | copy-start | bytes 49156
  196.4 21.4 %copy-start.90 = (f32[32]{0:T(128)S(1)}, f32[32]{0:T(128)}, u32[]{:S(2)}) copy-start(f32[32]{0:T(128)} %copy-done.88) | copy-start | bytes 388
  196.4 21.6 %copy-start.50 = (pred[128,128]{0,1:T(8,128)(4,1)S(1)}, pred[128,128]{0,1:T(8,128)(4,1)}, u32[]{:S(2)}) copy-start(pred[128,128]{0,1:T(8,128)(4,1)} %copy-done.49) | copy-start | bytes 49156
  212.2 6.1 %copy-start.5 = (bf16[128,2560]{1,0:T(8,128)(2,1)}, bf16[128,2560]{1,0:T(8,128)(2,1)S(1)}, u32[]{:S(2)}) copy-start(bf16[128,2560]{1,0:T(8,128)(2,1)S(1)} %all_gather.28) | copy-start | bytes 1966084
  212.2 27.1 %slice-start.3 = ((s8[5242880]{0:T(1024)(128)(4,1)}), s8[4194304]{0:T(1024)(128)(4,1)S(1)}, s32[]{:S(2)}) async-start(s8[5242880]{0:T(1024)(128)(4,1)} %bitcast.493), calls=%async_computation.15 | async-start | bytes 8388608
  213.2 7.1 %copy-start.29 = (f32[128,1,10,64]{0,3,2,1:T(8,128)}, f32[128,1,10,64]{0,3,2,1:T(8,128)S(1)}, u32[]{:S(2)}) copy-start(f32[128,1,10,64]{0,3,2,1:T(8,128)S(1)} %convolution_bitcast_fusion.5) | copy-start | bytes 983044
  213.4 6.9 %collective-permute-start.1 = (bf16[32,2560]{1,0:T(8,128)(2,1)S(1)}, bf16[32,2560]{1,0:T(8,128)(2,1)S(1)}, u32[]{:S(2)}, u32[]{:S(2)}) collective-permute-start(bf16[32,2560]{1,0:T(8,128)(2,1)S(1)} %get-tuple-element.52), channel_id=1, source_target_pairs={{8,0},{16,8},{24,16},{9,1},{17,9},{25,17},{10,2},{18,10},{26,18},{... | collective-permute-start | bytes 491528 | tf_op jit(solution)/shard_map/ppermute | solution.py:17
  214.8 5.5 %collective-permute-start = (bf16[32,2560]{1,0:T(8,128)(2,1)S(1)}, bf16[32,2560]{1,0:T(8,128)(2,1)S(1)}, u32[]{:S(2)}, u32[]{:S(2)}) collective-permute-start(bf16[32,2560]{1,0:T(8,128)(2,1)S(1)} %get-tuple-element.53), channel_id=1, source_target_pairs={{0,8},{8,16},{16,24},{1,9},{9,17},{17,25},{2,10},{10,18},{18,26},{... | collective-permute-start | bytes 491528 | tf_op jit(solution)/shard_map/ppermute | solution.py:17
  218.0 20.3 %copy-start.68 = (bf16[128,32]{0,1:T(8,128)(2,1)}, bf16[128,32]{0,1:T(8,128)(2,1)S(1)}, u32[]{:S(2)}) copy-start(bf16[128,32]{0,1:T(8,128)(2,1)S(1)} %get-tuple-element.104) | copy-start | bytes 24580
  218.0 20.3 %copy-start.70 = (bf16[128,32]{0,1:T(8,128)(2,1)}, bf16[128,32]{0,1:T(8,128)(2,1)S(1)}, u32[]{:S(2)}) copy-start(bf16[128,32]{0,1:T(8,128)(2,1)S(1)} %get-tuple-element.105) | copy-start | bytes 24580
  218.4 23.0 %copy-start.84 = (f32[8,128]{1,0:T(8,128)}, f32[8,128]{1,0:T(8,128)S(1)}, u32[]{:S(2)}) copy-start(f32[8,128]{1,0:T(8,128)S(1)} %fusion.53) | copy-start | bytes 12292
  219.6 18.8 %copy-start.78 = (f32[8,128]{1,0:T(8,128)}, f32[8,128]{1,0:T(8,128)S(1)}, u32[]{:S(2)}) copy-start(f32[8,128]{1,0:T(8,128)S(1)} %get-tuple-element.125) | copy-start | bytes 12292
  261.5 10.7 %slice-start = ((s8[6553600]{0:T(1024)(128)(4,1)}), s8[2359296]{0:T(1024)(128)(4,1)S(1)}, s32[]{:S(2)}) async-start(s8[6553600]{0:T(1024)(128)(4,1)} %bitcast.467), calls=%async_computation.12 | async-start | bytes 4718592
  266.7 4.0 copy-start.30
  266.8 4.0 copy-start.48
  266.8 4.0 copy-start.58
  266.8 5.4 %slice-start.1 = ((s8[6553600]{0:T(1024)(128)(4,1)}), s8[4194304]{0:T(1024)(128)(4,1)S(1)}, s32[]{:S(2)}) async-start(s8[6553600]{0:T(1024)(128)(4,1)} %bitcast.467), calls=%async_computation.13 | async-start | bytes 8388608
  274.2 47.5 %reduce-scatter.11.cloned.1.call-start = ((), (), s32[]{:S(2)}) async-start(), calls=%async_computation.8 | async-start | bytes 819200 | tf_op jit(solution)/shard_map/reduce_scatter | solution.py:166
  276.0 5.2 %copy-start.18 = (bf16[128,2560]{1,0:T(8,128)(2,1)S(1)}, bf16[128,2560]{1,0:T(8,128)(2,1)}, u32[]{:S(2)}) copy-start(bf16[128,2560]{1,0:T(8,128)(2,1)} %copy-done.17) | copy-start | bytes 1966084
  284.4 105.5 %reduce-scatter.17.cloned.1.call-start = ((), (), s32[]{:S(2)}) async-start(), calls=%async_computation.11 | async-start | bytes 7864320 | tf_op jit(solution)/shard_map/reduce_scatter | solution.py:209
  292.6 179.9 %reduce-scatter.15.cloned.1.call-start = ((), (), s32[]{:S(2)}) async-start(), calls=%async_computation.10 | async-start | bytes 9830400 | tf_op jit(solution)/shard_map/reduce_scatter | solution.py:206
  301.4 20.3 %copy-start.2 = (bf16[2,2,1,1,32,2560]{5,4,3,2,1,0:T(8,128)(2,1)S(1)}, bf16[2,2,1,1,32,2560]{5,4,3,2,1,0:T(8,128)(2,1)}, u32[]{:S(2)}) copy-start(bf16[2,2,1,1,32,2560]{5,4,3,2,1,0:T(8,128)(2,1)} %param.6) | copy-start | bytes 1966084
  301.4 20.3 %copy-start.44 = (f32[2560]{0:T(1024)S(1)}, f32[2560]{0:T(1024)}, u32[]{:S(2)}) copy-start(f32[2560]{0:T(1024)} %copy-done.42) | copy-start | bytes 30724
  301.4 20.3 %copy-start.97 = (f32[32]{0:T(128)S(1)}, f32[32]{0:T(128)}, u32[]{:S(2)}) copy-start(f32[32]{0:T(128)} %copy-done.96) | copy-start | bytes 388
  301.4 20.3 %copy-start.99 = (f32[32]{0:T(128)S(1)}, f32[32]{0:T(128)}, u32[]{:S(2)}) copy-start(f32[32]{0:T(128)} %copy-done.98) | copy-start | bytes 388
  301.4 21.6 %copy-start.75 = (f32[2560]{0:T(1024)S(1)}, f32[2560]{0:T(1024)}, u32[]{:S(2)}) copy-start(f32[2560]{0:T(1024)} %get-tuple-element.43) | copy-start | bytes 30724
  301.4 21.7 %copy-start.74 = (f32[2560]{0:T(1024)S(1)}, f32[2560]{0:T(1024)}, u32[]{:S(2)}) copy-start(f32[2560]{0:T(1024)} %get-tuple-element.34) | copy-start | bytes 30724
  301.5 57.7 %copy-start.22 = (bf16[32,2560]{1,0:T(8,128)(2,1)S(1)}, bf16[32,2560]{1,0:T(8,128)(2,1)}, u32[]{:S(2)}) copy-start(bf16[32,2560]{1,0:T(8,128)(2,1)} %copy-done.21) | copy-start | bytes 491524
  301.5 57.7 %copy-start.24 = (bf16[32,2560]{1,0:T(8,128)(2,1)S(1)}, bf16[32,2560]{1,0:T(8,128)(2,1)}, u32[]{:S(2)}) copy-start(bf16[32,2560]{1,0:T(8,128)(2,1)} %copy-done.23) | copy-start | bytes 491524
  (48 other events, 99.7 us)
Sparse Core Ops, SparseCore 0:
  127.1 23.3 reduce-scatter.8
  153.4 21.2 reduce-scatter.6
  274.4 23.2 reduce-scatter.12
  300.4 21.2 reduce-scatter.10
  324.4 65.4 reduce-scatter.16
  392.6 79.8 reduce-scatter.14
where the time goes:
time: 481 us; the launch traced here: 479 us
  blocking collectives  171 us (36%)
  waiting for transfers between devices  168 us (35%)
  matrix products  64 us (13%)
  local copies, waits for them, and re-layouts  32.3 us (7%)
  other arithmetic  23 us (5%)
  between operations  15.6 us (3%)
  starting transfers between devices  4.93 us (1%)
    reduce_scatter x1, waiting for transfers between devices, local(): lax.psum_scatter(jnp.stack(qkv_sums).astype(jnp.bfloat16), 'dp', scatter_...  82.6 us
    all_gather x4, blocking collectives, local(): input_grad_full = lax.all_gather(grad_output, 'tensor', axis=0, tiled=True)  68.9 us
    all_gather x4, blocking collectives, local(): input_normed = lax.all_gather(normed_own, 'tensor', axis=0, tiled=True)  66.6 us
    reduce_scatter x4, waiting for transfers between devices, local(): lax.psum_scatter(lax.dot_general(input_grad_projected, weight_qkv[member]...  56.8 us
    psum x1, blocking collectives, local(): gain_total = lax.psum(jnp.stack(gain_totals), ('tensor', 'dp'))  36 us
    reduce_scatter x1, waiting for transfers between devices, local(): lax.psum_scatter(jnp.stack(out_sums).astype(jnp.bfloat16), 'dp', scatter_...  28.5 us
    dot_general x3, local copies, waits for them, and re-layouts, local(): jnp.dot(input_normed, weight_qkv[member], preferred_element_type=jnp.floa...  15.9 us
    dot_general x4, matrix products, local(): lax.dot_general(input_grad_projected, weight_qkv[member], contract_cols,...  14 us
  transfers between devices with their start and end apart: 8, of which 5 were waited for; matrix products, arithmetic and copies ran while one was open for 8% of the time, Pallas kernels for 0%

commit v1 on v0

--- a/solution.py
+++ b/solution.py
@@ -97,7 +97,10 @@
             )
             unit_rows = inputs_float * inverse
             normed_own = (unit_rows * gain_rows[member]).astype(jnp.bfloat16)
-            input_normed = lax.all_gather(normed_own, "tensor", axis=0, tiled=True)
+            size = lax.axis_size("tensor")
+            blocks = jnp.stack([normed_own for _ in range(size)])
+            blocks = lax.all_to_all(blocks, "tensor", split_axis=0, concat_axis=0)
+            input_normed = jnp.concatenate(blocks, axis=0)
             input_grad_full = lax.all_gather(grad_output, "tensor", axis=0, tiled=True)
             projected = jnp.dot(
                 input_normed, weight_qkv[member], preferred_element_type=jnp.float32

time: 481 us -> 464 us (0.965)
  blocking collectives: 171 us -> 136 us
  starting transfers between devices: 4.93 us -> 25.6 us
    all_gather x4 -> x0, blocking collectives: 66.6 us -> none  [local(): input_normed = lax.all_gather(normed_own, 'tensor', axis=0, tiled=True)]
    all_gather x4, blocking collectives: 68.9 us -> 100 us  [local(): input_grad_full = lax.all_gather(grad_output, 'tensor', axis=0, tiled=True)]
    all_to_all x0 -> x4, starting transfers between devices: none -> 20.2 us  [local(): blocks = lax.all_to_all(blocks, 'tensor', split_axis=0, concat_axis=0)]
    unnamed x208 -> x110, local copies, waits for them, and re-layouts: 10.3 us -> 7 us
  transfers between devices with their start and end apart: 8 -> 12, of which waited for: 5 -> 5; matrix products, arithmetic and copies ran while one was open for 8% -> 18% of each run, Pallas kernels for 0% -> 0%
where the time goes in v1:
time: 464 us; the launch traced here: 463 us
  waiting for transfers between devices  167 us (36%)
  blocking collectives  136 us (29%)
  matrix products  62.4 us (13%)
  local copies, waits for them, and re-layouts  33.9 us (7%)
  starting transfers between devices  25.6 us (6%)
  other arithmetic  22 us (5%)
  between operations  15.2 us (3%)
    all_gather x4, blocking collectives, local(): input_grad_full = lax.all_gather(grad_output, 'tensor', axis=0, tiled=True)  100 us
    reduce_scatter x1, waiting for transfers between devices, local(): lax.psum_scatter(jnp.stack(qkv_sums).astype(jnp.bfloat16), 'dp', scatter_...  82.6 us
    reduce_scatter x4, waiting for transfers between devices, local(): lax.psum_scatter(lax.dot_general(input_grad_projected, weight_qkv[member]...  56.1 us
    psum x1, blocking collectives, local(): gain_total = lax.psum(jnp.stack(gain_totals), ('tensor', 'dp'))  36.1 us
    reduce_scatter x1, waiting for transfers between devices, local(): lax.psum_scatter(jnp.stack(out_sums).astype(jnp.bfloat16), 'dp', scatter_...  28.5 us
    all_to_all x4, starting transfers between devices, local(): blocks = lax.all_to_all(blocks, 'tensor', split_axis=0, concat_axis=0)  20.2 us
    dot_general x3, local copies, waits for them, and re-layouts, local(): jnp.dot(input_normed, weight_qkv[member], preferred_element_type=jnp.floa...  16.2 us
    dot_general x4, matrix products, local(): lax.dot_general(input_grad_full, weight_out[member], contract_cols, prefe...  12.3 us
  transfers between devices with their start and end apart: 12, of which 5 were waited for; matrix products, arithmetic and copies ran while one was open for 18% of the time, Pallas kernels for 0%

profile of v1, /device:TPU:0, one launch (start us, length us, event | category | flops | bytes accessed | tf_op | source)
XLA Modules:
  0.0 462.5 jit_solution(14137303537779229546)
XLA Ops:
  7.2 1.2 fusion.91
  9.2 1.2 fusion.88
  10.4 0.9 stack.84
  11.3 6.3 %all-to-all-start = ((bf16[4,32,2560]{2,1,0:T(8,128)(2,1)}), bf16[4,32,2560]{2,1,0:T(8,128)(2,1)S(1)}, u32[]{:S(2)}, u32[]{:S(2)}) async-start(bf16[4,32,2560]{2,1,0:T(8,128)(2,1)} %stack.84), calls=%async_computation | async-start | bytes 1310720 | tf_op jit(solution)/shard_map/all_to_all | solution.py:102
  17.6 28.7 %all-gather = bf16[1,1,1,128,2560]{4,3,2,1,0:T(8,128)(2,1)S(1)} all-gather(bf16[1,1,1,32,2560]{4,3,2,1,0:T(8,128)(2,1)S(1)} %get-tuple-element.68), channel_id=2, replica_groups=mesh['section'=4,'tensor'=4,'dp'=2] {'tensor'}, dimensions={3}, use_global_device_ids=true | all-gather | bytes 819200 | tf_op jit(solution)/shard_map/all_gather | solution.py:104
  46.3 2.9 fusion.32
  49.3 16.6 %all-gather.1 = bf16[1,1,1,128,2560]{4,3,2,1,0:T(8,128)(2,1)S(1)} all-gather(bf16[1,1,1,32,2560]{4,3,2,1,0:T(8,128)(2,1)S(1)} %get-tuple-element.69), channel_id=3, replica_groups=mesh['section'=4,'tensor'=4,'dp'=2] {'tensor'}, dimensions={3}, use_global_device_ids=true | all-gather | bytes 819200 | tf_op jit(solution)/shard_map/all_gather | solution.py:104
  65.9 6.5 %slice_bitcast_fusion.1 = (bf16[640,2560]{0,1:T(8,128)(2,1)}, bf16[640,2560]{0,1:T(8,128)(2,1)}) fusion(bf16[2,1,2560,640]{3,2,1,0:T(8,128)(2,1)} %param.9), kind=kLoop, calls=%fused_computation.30 | loop fusion | bytes 13107200 | tf_op jit(solution)/shard_map/dot_general | solution.py:105
  72.4 0.9 stack.86
  73.3 4.9 %all-to-all-start.1 = ((bf16[4,32,2560]{2,1,0:T(8,128)(2,1)}), bf16[4,32,2560]{2,1,0:T(8,128)(2,1)}, u32[]{:S(2)}, u32[]{:S(2)}) async-start(bf16[4,32,2560]{2,1,0:T(8,128)(2,1)} %stack.86), calls=%async_computation.2 | async-start | bytes 1310720 | tf_op jit(solution)/shard_map/all_to_all | solution.py:102
  78.2 2.7 fusion.38
  82.4 4.0 copy.39
  86.4 5.7 %copy.44 = bf16[640,2560]{1,0:T(8,128)(2,1)} copy(bf16[640,2560]{0,1:T(8,128)(2,1)} %get-tuple-element.51) | data formatting | bytes 6553600 | tf_op jit(solution)/shard_map/dot_general | solution.py:105
  92.3 2.1 convolution_bitcast_fusion.7
  95.1 3.2 convolution_bitcast_fusion.6
  102.5 2.0 convolution_convert_fusion.2
  104.6 1.3 convolution_bitcast_fusion.18
  106.7 4.0 convolution_convert_fusion.3
  110.7 1.9 convolution_convert_fusion.6
  112.6 16.2 %reduce-scatter.9.cloned.1.call-done = bf16[32,2560]{1,0:T(8,128)(2,1)} async-done(((bf16[128,2560]{1,0:T(8,128)(2,1)}), bf16[32,2560]{1,0:T(8,128)(2,1)}) %reduce-scatter.9.cloned.1.call-update) | async-done | bytes 163856 | tf_op jit(solution)/shard_map/reduce_scatter | solution.py:169
  128.8 24.1 %reduce-scatter.7.cloned.1.call-done = bf16[32,2560]{1,0:T(8,128)(2,1)} async-done(((bf16[128,2560]{1,0:T(8,128)(2,1)}), bf16[32,2560]{1,0:T(8,128)(2,1)}) %reduce-scatter.7.cloned.1.call-update) | async-done | bytes 163856 | tf_op jit(solution)/shard_map/reduce_scatter | solution.py:169
  152.9 1.7 fusion.90
  154.7 2.4 fusion.87
  157.1 1.3 collective-permute-start.1
  158.4 3.7 collective-permute-start
  162.1 2.0 convolution_convert_fusion.7
  164.0 0.9 stack.92
  164.9 4.2 all-to-all-start.3
  169.1 0.9 bitcast_select_fusion
  170.7 27.6 %all_gather.15 = bf16[128,2560]{1,0:T(8,128)(2,1)S(1)} all-gather(bf16[32,2560]{1,0:T(8,128)(2,1)S(1)} %bitcast_select_fusion), channel_id=1, replica_groups=mesh['section'=4,'tensor'=4,'dp'=2] {'tensor'}, dimensions={0}, use_global_device_ids=true | all-gather | bytes 819200 | tf_op jit(solution)/shard_map/all_gather | solution.py:104
  198.3 0.8 copy-done.8
  199.2 3.3 fusion.41
  202.5 1.7 copy.55
  204.2 1.6 broadcast_select_fusion
  205.8 1.8 stack.90
  207.6 4.8 %all-to-all-start.2 = ((bf16[4,32,2560]{2,1,0:T(8,128)(2,1)}), bf16[4,32,2560]{2,1,0:T(8,128)(2,1)}, u32[]{:S(2)}, u32[]{:S(2)}) async-start(bf16[4,32,2560]{2,1,0:T(8,128)(2,1)} %stack.90), calls=%async_computation.4 | async-start | bytes 1310720 | tf_op jit(solution)/shard_map/all_to_all | solution.py:102
  212.4 27.1 %all_gather.14 = bf16[128,2560]{1,0:T(8,128)(2,1)S(1)} all-gather(bf16[32,2560]{1,0:T(8,128)(2,1)} %broadcast_select_fusion), channel_id=1, replica_groups=mesh['section'=4,'tensor'=4,'dp'=2] {'tensor'}, dimensions={0}, use_global_device_ids=true | all-gather | bytes 819200 | tf_op jit(solution)/shard_map/all_gather | solution.py:104
  239.5 0.9 copy-done.10
  240.4 3.3 fusion.35
  243.7 1.7 copy.51
  245.4 3.1 convolution_bitcast_fusion.4
  249.9 2.1 convolution_bitcast_fusion.5
  255.9 2.0 convolution_convert_fusion
  258.4 1.1 convolution_convert_fusion.4
  259.4 4.0 convolution_convert_fusion.1
  263.4 3.1 fusion.189
  266.6 3.6 fusion.3
  270.3 1.0 convolution_convert_fusion.5
  271.3 0.8 fusion.188
  272.4 0.9 fusion.2
  273.2 2.8 pad_maximum_fusion.1
  277.0 2.2 fusion.186
  279.2 1.0 fusion
  280.3 2.2 fusion.187
  282.4 2.1 fusion.1
  284.6 3.4 pad_maximum_fusion
  288.0 1.0 maximum_bitcast_fusion.1
  289.1 15.8 %reduce-scatter.11.cloned.1.call-done = bf16[32,2560]{1,0:T(8,128)(2,1)} async-done(((bf16[128,2560]{1,0:T(8,128)(2,1)}), bf16[32,2560]{1,0:T(8,128)(2,1)}) %reduce-scatter.11.cloned.1.call-update) | async-done | bytes 163856 | tf_op jit(solution)/shard_map/reduce_scatter | solution.py:169
  304.9 1.4 fusion.98
  306.4 36.1 %psum.7 = f32[2,1,2560]{2,1,0:T(1,128)} all-reduce(f32[2,1,2560]{2,1,0:T(1,128)S(1)} %broadcast_in_dim.33), channel_id=1, replica_groups=mesh['section'=4,'tensor'=4,'dp'=2] {'tensor','dp'}, use_global_device_ids=true, to_apply=%region_30.31 | all-reduce | flops 5120 | bytes 40960 | tf_op jit(solution)/shard_map/psum | solution.py:216
  342.4 1.2 fusion.116
  343.7 0.9 maximum_bitcast_fusion
  344.6 28.5 %reduce-scatter.17.cloned.1.call-done = bf16[2,256,2560]{2,1,0:T(8,128)(2,1)} async-done(((bf16[2,512,2560]{2,1,0:T(8,128)(2,1)}), bf16[2,256,2560]{2,1,0:T(8,128)(2,1)}) %reduce-scatter.17.cloned.1.call-update) | async-done | bytes 2621456 | tf_op jit(solution)/shard_map/reduce_scatter | solution.py:212
  373.1 82.6 %reduce-scatter.15.cloned.1.call-done = bf16[2,1280,640]{2,1,0:T(8,128)(2,1)} async-done(((bf16[2,2560,640]{2,1,0:T(8,128)(2,1)}), bf16[2,1280,640]{2,1,0:T(8,128)(2,1)}) %reduce-scatter.15.cloned.1.call-update) | async-done | bytes 3276816 | tf_op jit(solution)/shard_map/reduce_scatter | solution.py:209
  (197 shorter events, 15.3 us)
Async XLA Ops:
  7.2 10.4 %copy-start.15 = (bf16[2,1,1,32,2560]{4,3,2,1,0:T(8,128)(2,1)S(1)}, bf16[2,1,1,32,2560]{4,3,2,1,0:T(8,128)(2,1)}, u32[]{:S(2)}) copy-start(bf16[2,1,1,32,2560]{4,3,2,1,0:T(8,128)(2,1)} %param.7) | copy-start | bytes 983044
  9.2 2.1 copy-start.43
  9.2 2.1 copy-start.45
  11.3 61.1 %all-to-all-start = ((bf16[4,32,2560]{2,1,0:T(8,128)(2,1)}), bf16[4,32,2560]{2,1,0:T(8,128)(2,1)S(1)}, u32[]{:S(2)}, u32[]{:S(2)}) async-start(bf16[4,32,2560]{2,1,0:T(8,128)(2,1)} %stack.84), calls=%async_computation | async-start | bytes 1310720 | tf_op jit(solution)/shard_map/all_to_all | solution.py:102
  46.3 26.0 %copy-start.5 = (bf16[1,1,1,128,2560]{4,3,2,1,0:T(8,128)(2,1)}, bf16[1,1,1,128,2560]{4,3,2,1,0:T(8,128)(2,1)S(1)}, u32[]{:S(2)}) copy-start(bf16[1,1,1,128,2560]{4,3,2,1,0:T(8,128)(2,1)S(1)} %all-gather) | copy-start | bytes 1966084
  65.9 12.3 %copy-start.7 = (bf16[1,1,1,128,2560]{4,3,2,1,0:T(8,128)(2,1)}, bf16[1,1,1,128,2560]{4,3,2,1,0:T(8,128)(2,1)S(1)}, u32[]{:S(2)}) copy-start(bf16[1,1,1,128,2560]{4,3,2,1,0:T(8,128)(2,1)S(1)} %all-gather.1) | copy-start | bytes 1966084
  72.4 10.0 %copy-start.1 = (bf16[4,32,2560]{2,1,0:T(8,128)(2,1)}, bf16[4,32,2560]{2,1,0:T(8,128)(2,1)S(1)}, u32[]{:S(2)}) copy-start(bf16[4,32,2560]{2,1,0:T(8,128)(2,1)S(1)} %all-to-all-done) | copy-start | bytes 1966084
  73.3 21.8 %all-to-all-start.1 = ((bf16[4,32,2560]{2,1,0:T(8,128)(2,1)}), bf16[4,32,2560]{2,1,0:T(8,128)(2,1)}, u32[]{:S(2)}, u32[]{:S(2)}) async-start(bf16[4,32,2560]{2,1,0:T(8,128)(2,1)} %stack.86), calls=%async_computation.2 | async-start | bytes 1310720 | tf_op jit(solution)/shard_map/all_to_all | solution.py:102
  78.2 50.6 %reduce-scatter.9.cloned.1.call-start = ((), (), s32[]{:S(2)}) async-start(), calls=%async_computation.11 | async-start | bytes 819200 | tf_op jit(solution)/shard_map/reduce_scatter | solution.py:169
  92.1 9.2 %copy-start.41 = (f32[32]{0:T(128)}, f32[32]{0:T(128)S(1)}, u32[]{:S(2)}) copy-start(f32[32]{0:T(128)S(1)} %negate_power_fusion) | copy-start | bytes 388
  94.4 0.7 copy-start.17
  95.1 3.4 copy-start.18
  95.1 3.8 copy-start.32
  98.3 2.2 copy-start.16
  98.9 1.0 copy-start.4
  98.9 1.4 copy-start.36
  99.0 3.3 slice-start
  100.1 1.0 copy-start.3
  100.1 1.0 copy-start.37
  100.2 0.9 copy-start.38
  100.2 2.3 slice-start.1
  104.5 48.4 %reduce-scatter.7.cloned.1.call-start = ((), (), s32[]{:S(2)}) async-start(), calls=%async_computation.10 | async-start | bytes 819200 | tf_op jit(solution)/shard_map/reduce_scatter | solution.py:169
  106.7 46.3 %copy-start.44 = (f32[32]{0:T(128)S(1)}, f32[32]{0:T(128)}, u32[]{:S(2)}) copy-start(f32[32]{0:T(128)} %copy-done.43) | copy-start | bytes 388
  106.7 46.3 %copy-start.46 = (f32[32]{0:T(128)S(1)}, f32[32]{0:T(128)}, u32[]{:S(2)}) copy-start(f32[32]{0:T(128)} %copy-done.45) | copy-start | bytes 388
  154.6 3.7 copy-start.47
  154.7 3.7 copy-start.49
  157.1 12.0 %collective-permute-start.1 = (bf16[32,2560]{1,0:T(8,128)(2,1)}, bf16[32,2560]{1,0:T(8,128)(2,1)}, u32[]{:S(2)}, u32[]{:S(2)}) collective-permute-start(bf16[32,2560]{1,0:T(8,128)(2,1)} %get-tuple-element.52), channel_id=1, source_target_pairs={{8,0},{16,8},{24,16},{9,1},{17,9},{25,17},{10,2},{18,10},{26,18},{... | collective-permute-start | bytes 491528 | tf_op jit(solution)/shard_map/ppermute | solution.py:17
  158.4 10.7 %collective-permute-start = (bf16[32,2560]{1,0:T(8,128)(2,1)S(1)}, bf16[32,2560]{1,0:T(8,128)(2,1)}, u32[]{:S(2)}, u32[]{:S(2)}) collective-permute-start(bf16[32,2560]{1,0:T(8,128)(2,1)S(1)} %get-tuple-element.53), channel_id=1, source_target_pairs={{0,8},{8,16},{16,24},{1,9},{9,17},{17,25},{2,10},{10,18},{18,26},{... | collective-permute-start | bytes 491528 | tf_op jit(solution)/shard_map/ppermute | solution.py:17
  164.9 40.9 %all-to-all-start.3 = ((bf16[4,32,2560]{2,1,0:T(8,128)(2,1)}), bf16[4,32,2560]{2,1,0:T(8,128)(2,1)}, u32[]{:S(2)}, u32[]{:S(2)}) async-start(bf16[4,32,2560]{2,1,0:T(8,128)(2,1)} %stack.92), calls=%async_computation.6 | async-start | bytes 1310720 | tf_op jit(solution)/shard_map/all_to_all | solution.py:102
  198.3 0.8 copy-start.8
  207.6 42.3 %all-to-all-start.2 = ((bf16[4,32,2560]{2,1,0:T(8,128)(2,1)}), bf16[4,32,2560]{2,1,0:T(8,128)(2,1)}, u32[]{:S(2)}, u32[]{:S(2)}) async-start(bf16[4,32,2560]{2,1,0:T(8,128)(2,1)} %stack.90), calls=%async_computation.4 | async-start | bytes 1310720 | tf_op jit(solution)/shard_map/all_to_all | solution.py:102
  212.4 76.6 %reduce-scatter.13.cloned.1.call-start = ((), (), s32[]{:S(2)}) async-start(), calls=%async_computation.13 | async-start | bytes 819200 | tf_op jit(solution)/shard_map/reduce_scatter | solution.py:169
  239.5 0.9 copy-start.10
  248.5 0.7 copy-start.20
  249.9 2.2 copy-start.21
  249.9 2.3 copy-start.31
  249.9 2.3 copy-start.42
  249.9 2.8 copy-start.33
  252.1 1.5 copy-start.19
  252.6 1.3 copy-start.35
  252.7 5.3 %copy-start.39 = (f32[8,128]{1,0:T(8,128)}, f32[8,128]{1,0:T(8,128)S(1)}, u32[]{:S(2)}) copy-start(f32[8,128]{1,0:T(8,128)S(1)} %fusion.53) | copy-start | bytes 12292
  252.7 2.6 slice-start.2
  254.0 1.9 slice-start.3
  255.0 3.0 copy-start.34
  255.3 3.0 copy-start.22
  258.0 46.9 %reduce-scatter.11.cloned.1.call-start = ((), (), s32[]{:S(2)}) async-start(), calls=%async_computation.12 | async-start | bytes 819200 | tf_op jit(solution)/shard_map/reduce_scatter | solution.py:169
  258.3 5.1 %copy-start.24 = (bf16[128,1,10,64]{0,3,2,1:T(8,128)(2,1)}, bf16[128,1,10,64]{0,3,2,1:T(8,128)(2,1)S(1)}, u32[]{:S(2)}) copy-start(bf16[128,1,10,64]{0,3,2,1:T(8,128)(2,1)S(1)} %pad_maximum_fusion.2) | copy-start | bytes 491524
  258.3 5.1 %copy-start.9 = (bf16[128,2560]{1,0:T(8,128)(2,1)S(1)}, bf16[128,2560]{1,0:T(8,128)(2,1)}, u32[]{:S(2)}) copy-start(bf16[128,2560]{1,0:T(8,128)(2,1)} %copy-done.8) | copy-start | bytes 1966084
  266.6 3.7 copy-start.40
  266.6 106.5 %reduce-scatter.17.cloned.1.call-start = ((), (), s32[]{:S(2)}) async-start(), calls=%async_computation.15 | async-start | bytes 7864320 | tf_op jit(solution)/shard_map/reduce_scatter | solution.py:212
  266.6 4.6 %copy-start.11 = (bf16[128,2560]{1,0:T(8,128)(2,1)S(1)}, bf16[128,2560]{1,0:T(8,128)(2,1)}, u32[]{:S(2)}) copy-start(bf16[128,2560]{1,0:T(8,128)(2,1)} %copy-done.10) | copy-start | bytes 1966084
  271.3 1.1 copy-start.6
  271.3 1.1 copy-start.30
  276.0 0.9 copy-start.25
  276.1 179.6 %reduce-scatter.15.cloned.1.call-start = ((), (), s32[]{:S(2)}) async-start(), calls=%async_computation.14 | async-start | bytes 9830400 | tf_op jit(solution)/shard_map/reduce_scatter | solution.py:209
  277.0 2.2 copy-start.2
  277.0 2.2 copy-start.29
  279.2 1.1 copy-start.23
  280.3 2.2 copy-start.27
  288.0 16.9 %copy-start = (bf16[2,2,1,1,32,2560]{5,4,3,2,1,0:T(8,128)(2,1)S(1)}, bf16[2,2,1,1,32,2560]{5,4,3,2,1,0:T(8,128)(2,1)}, u32[]{:S(2)}) copy-start(bf16[2,2,1,1,32,2560]{5,4,3,2,1,0:T(8,128)(2,1)} %param.6) | copy-start | bytes 1966084
  288.0 16.9 %copy-start.48 = (f32[32]{0:T(128)S(1)}, f32[32]{0:T(128)}, u32[]{:S(2)}) copy-start(f32[32]{0:T(128)} %copy-done.47) | copy-start | bytes 388
  288.0 16.9 %copy-start.50 = (f32[32]{0:T(128)S(1)}, f32[32]{0:T(128)}, u32[]{:S(2)}) copy-start(f32[32]{0:T(128)} %copy-done.49) | copy-start | bytes 388
  288.0 54.4 %copy-start.13 = (bf16[32,2560]{1,0:T(8,128)(2,1)S(1)}, bf16[32,2560]{1,0:T(8,128)(2,1)}, u32[]{:S(2)}) copy-start(bf16[32,2560]{1,0:T(8,128)(2,1)} %copy-done.12) | copy-start | bytes 491524
  288.0 54.4 %copy-start.14 = (bf16[32,2560]{1,0:T(8,128)(2,1)S(1)}, bf16[32,2560]{1,0:T(8,128)(2,1)}, u32[]{:S(2)}) copy-start(bf16[32,2560]{1,0:T(8,128)(2,1)} %broadcast_select_fusion) | copy-start | bytes 491524
  (3 other events, 2.0 us)
Sparse Core Ops, SparseCore 0:
  104.7 24.0 reduce-scatter.8
  131.6 21.2 reduce-scatter.6
  258.1 23.2 reduce-scatter.12
  283.6 21.2 reduce-scatter.10
  307.6 65.4 reduce-scatter.16
  375.8 79.8 reduce-scatter.14
